TPU v7x, 32 devices: a whole 2x2x4 slice. The times are simulated.
32 devices in a mesh: gx: 4 (over y, x), gy: 8 (over z, core).
Axes of the slice: x: 2, y: 2, z: 4, core: 2. Of those that a mesh axis runs over, the one named last changes fastest.
Arguments:
- replay_deter: float32 [8192, 2048], P(('gx', 'gy')), may hold values from -1 to 1
- replay_stoch: int32 [8192, 32], P(('gx', 'gy')), may hold values from 0 to 31
- send_rows: int32 [1024, 8], P(('gx', 'gy')), may hold values from 0 to 255
- send_counts: int32 [32, 32], P(('gx', 'gy')), may hold values from 0 to 8, as said below
- actions: int32 [8192, 4], P(('gx', 'gy')), may hold values from 0 to 17
- samples: int32 [8192, 4, 32], P(('gx', 'gy')), may hold values from 0 to 31
- w_stoch: bfloat16 [1024, 6144], P('gy'), may hold values from -1 to 1
- w_deter: bfloat16 [4, 512, 1536], P(None, 'gy'), may hold values from -0.25 to 0.25
- act_table: bfloat16 [18, 6144], replicated, may hold values from -3 to 3
- w_prior: bfloat16 [2048, 1024], P('gy'), may hold values from -0.037353516 to 0.037353516
Outputs:
- imagined: bfloat16 [8192, 4, 2048], P(('gx', 'gy'))
- log_prob: float32 [8192, 4, 32], P(('gx', 'gy'))
Inputs may be any that keep to these rules, and one draw needn't show every extreme that they name: `send_rows`: entries past a destination's count are unused. `send_counts`: each source's counts sum to exactly 128; every source sends 8 rows to some owner, and some owner receives 8 rows from every source.
All inputs are finite; a program needn't handle non-finite values.
Results may differ from a plain program's by a relative error of at most 0.0022.
Values may be sent and summed in bfloat16 or wider, within the bound.
No kernel may reach another device: no remote copies, remote signals or barrier semaphores. Data moves between devices by JAX's collectives and lax.ppermute only.
A program may use at most 128 MiB of HBM per device.

v0:
```python
import jax
import jax.numpy as jnp
from jax import lax
from jax.sharding import PartitionSpec as P

GROUPS = 32
CLASSES = 32
STEPS = 4


def gate_inputs(stoch, action, actions_count):
    rows = stoch.shape[0]
    onehot = (
        (stoch[:, :, None] == jnp.arange(CLASSES, dtype=jnp.int32)[None, None, :])
        .reshape(rows, GROUPS * CLASSES)
        .astype(jnp.bfloat16)
    )
    act_hot = (action[:, None] == jnp.arange(actions_count, dtype=jnp.int32)[None, :]).astype(
        jnp.bfloat16
    )
    return (onehot, act_hot)


def imagine(start, first, acts, samps, stoch_full, deter_full, act_table):
    blocks = deter_full.shape[0]
    width = deter_full.shape[1]
    pieces = [start[:, b * width : (b + 1) * width] for b in range(blocks)]
    stoch = first
    states = []
    for step in range(STEPS):
        onehot, act_hot = gate_inputs(stoch, acts[:, step], act_table.shape[0])
        input_term = jnp.dot(onehot, stoch_full, preferred_element_type=jnp.float32) + jnp.dot(
            act_hot, act_table, preferred_element_type=jnp.float32
        )
        fresh = []
        for b in range(blocks):
            before = pieces[b]
            gates = input_term[:, 3 * width * b : 3 * width * (b + 1)] + jnp.dot(
                before.astype(jnp.bfloat16), deter_full[b], preferred_element_type=jnp.float32
            )
            reset = jax.nn.sigmoid(gates[:, :width])
            cand = jnp.tanh(reset * gates[:, width : 2 * width])
            update = jax.nn.sigmoid(gates[:, 2 * width :] - 1.0)
            fresh.append(update * cand + (1.0 - update) * before)
        pieces = fresh
        states.append(jnp.concatenate(pieces, 1).astype(jnp.bfloat16))
        stoch = samps[:, step]
    return jnp.stack(states, 1)


def on_device(
    replay_deter,
    replay_stoch,
    send_rows,
    send_counts,
    actions,
    samples,
    w_stoch,
    w_deter,
    act_table,
    w_prior,
):
    peers, cap = send_rows.shape
    slots = peers * cap
    deter = replay_deter.shape[1]
    stoch_full = lax.all_gather(w_stoch, "gy", axis=0, tiled=True)
    deter_full = lax.all_gather(w_deter, "gy", axis=1, tiled=True)
    outgoing = (jnp.arange(cap, dtype=jnp.int32)[None, :] < send_counts[0][:, None]).astype(
        jnp.int32
    )
    start = replay_deter[send_rows]
    first = replay_stoch[send_rows]
    start, first, live = (
        lax.all_to_all(start, ("gx", "gy"), split_axis=0, concat_axis=0, tiled=True),
        lax.all_to_all(first, ("gx", "gy"), split_axis=0, concat_axis=0, tiled=True),
        lax.all_to_all(outgoing, ("gx", "gy"), split_axis=0, concat_axis=0, tiled=True),
    )
    live = live.reshape(slots)
    states = imagine(
        start.reshape(slots, deter),
        first.reshape(slots, GROUPS),
        actions,
        samples,
        stoch_full,
        deter_full,
        act_table,
    )
    states = jnp.where(live[:, None, None] > 0, states, jnp.zeros_like(states))
    prior_full = lax.all_gather(w_prior, "gy", axis=0, tiled=True)
    logits = jnp.dot(
        states.reshape(slots * STEPS, deter), prior_full, preferred_element_type=jnp.float32
    )
    logits = logits.reshape(slots, STEPS, GROUPS, CLASSES)
    totals = jnp.log(jnp.sum(jnp.exp(logits), -1))
    hits = samples[..., None] == jnp.arange(CLASSES, dtype=jnp.int32)
    picked = jnp.sum(jnp.where(hits, logits, jnp.zeros_like(logits)), -1)
    log_prob = jnp.where(live[:, None, None] > 0, picked - totals, jnp.zeros_like(totals))
    return (states, log_prob)


def solution(mesh):
    in_specs = (
        P(("gx", "gy"), None),
        P(("gx", "gy"), None),
        P(("gx", "gy"), None),
        P(("gx", "gy"), None),
        P(("gx", "gy"), None),
        P(("gx", "gy"), None, None),
        P("gy", None),
        P(None, "gy", None),
        P(),
        P("gy", None),
    )
    out_specs = (P(("gx", "gy"), None, None), P(("gx", "gy"), None, None))
    return jax.shard_map(
        on_device, mesh=mesh, in_specs=in_specs, out_specs=out_specs, check_vma=False
    )
```

profile of v0, /device:TPU:0, one launch (start us, length us, event | category | flops | bytes accessed | tf_op | source)
XLA Modules:
  0.0 338.7 jit_solution(16087413320578995944)
XLA Ops:
  10.8 7.3 %all-to-all-start = ((s32[32,1,8]{2,1,0:T(1,128)}), s32[32,1,8]{2,1,0:T(1,128)S(1)}, u32[]{:S(2)}, u32[]{:S(2)}) async-start(s32[32,1,8]{2,1,0:T(1,128)} %compare_convert_fusion), calls=%async_computation | async-start | bytes 32768 | tf_op jit(solution)/shard_map/all_to_all | solution.py:76
  21.3 3.9 %all-to-all-done = s32[32,1,8]{2,1,0:T(1,128)S(1)} async-done(((s32[32,1,8]{2,1,0:T(1,128)}), s32[32,1,8]{2,1,0:T(1,128)S(1)}, u32[]{:S(2)}, u32[]{:S(2)}) %all-to-all-start) | async-done | bytes 1056 | tf_op jit(solution)/shard_map/all_to_all | solution.py:76
  25.2 2.6 all-to-all-start.1
  27.8 2.7 gather_fusion.1
  30.5 5.0 %all-to-all-done.1 = s32[32,1,256]{2,1,0:T(1,128)S(1)} async-done(((s32[32,1,256]{2,1,0:T(1,128)}), s32[32,1,256]{2,1,0:T(1,128)S(1)}, u32[]{:S(2)}, u32[]{:S(2)}) %all-to-all-start.1) | async-done | bytes 32800 | tf_op jit(solution)/shard_map/all_to_all | solution.py:75
  35.4 2.7 all-to-all-start.2
  41.3 41.9 %all-gather.8.cloned.1.call-done = bf16[2048,1024]{1,0:T(8,128)(2,1)} async-done(((bf16[256,1024]{1,0:T(8,128)(2,1)}), bf16[2048,1024]{1,0:T(8,128)(2,1)}) %all-gather.8.cloned.1.call-update) | async-done | bytes 4194320 | tf_op jit(solution)/shard_map/all_gather | solution.py:89
  83.2 6.5 %copy.26 = bf16[1024,2048]{1,0:T(8,128)(2,1)} copy(bf16[1024,2048]{0,1:T(8,128)(2,1)} %bitcast.116) | data formatting | bytes 8388608 | tf_op jit(solution)/shard_map/dot_general | solution.py:90
  89.7 116.9 %all-gather.4.cloned.1.call-done = bf16[1024,6144]{1,0:T(8,128)(2,1)} async-done(((bf16[128,6144]{1,0:T(8,128)(2,1)}), bf16[1024,6144]{1,0:T(8,128)(2,1)}) %all-gather.4.cloned.1.call-update) | async-done | bytes 12582928 | tf_op jit(solution)/shard_map/all_gather | solution.py:66
  206.6 7.0 %fusion.199 = f32[256,6144]{1,0:T(8,128)S(1)} fusion(pred[256,1024]{0,1:T(32,128)(4,1)S(1)} %get-tuple-element.50, bf16[1024,6144]{1,0:T(8,128)(2,1)} %all-gather.4.cloned.1.call-done), kind=kOutput, calls=%fused_computation.297 | convolution fusion | flops 3221225472 | bytes 19136512 | tf_op jit(solution)/shard_map/dot_general | solution.py:32
  213.6 3.7 %convolution_add_fusion.3 = f32[256,6144]{1,0:T(8,128)} fusion(f32[256,6144]{1,0:T(8,128)S(1)} %fusion.199, bf16[18,6144]{1,0:T(8,128)(2,1)S(1)} %copy-done.3, s32[256]{0:T(256)S(1)} %bitcast.122), kind=kOutput, calls=%fused_computation.5 | convolution fusion | flops 58200576 | bytes 12805120 | tf_op jit(solution)/shard_map/dot_general | solution.py:32
  217.3 3.6 %fusion.200 = f32[256,6144]{1,0:T(8,128)S(1)} fusion(pred[256,1024]{0,1:T(32,128)(4,1)S(1)} %get-tuple-element.48, bf16[1024,6144]{1,0:T(8,128)(2,1)S(1)} %bitcast.104), kind=kOutput, calls=%fused_computation.298 | convolution fusion | flops 3221225472 | bytes 19136512 | tf_op jit(solution)/shard_map/dot_general | solution.py:32
  221.0 3.6 %convolution_add_fusion.2 = f32[256,6144]{1,0:T(8,128)} fusion(f32[256,6144]{1,0:T(8,128)S(1)} %fusion.200, bf16[18,6144]{1,0:T(8,128)(2,1)S(1)} %copy-done.3, s32[256]{0:T(256)S(1)} %bitcast.121), kind=kOutput, calls=%fused_computation.4 | convolution fusion | flops 58200576 | bytes 12805120 | tf_op jit(solution)/shard_map/dot_general | solution.py:32
  224.6 47.0 %all-gather.6.cloned.1.call-done = bf16[4,512,1536]{2,1,0:T(8,128)(2,1)} async-done(((bf16[4,64,1536]{2,1,0:T(8,128)(2,1)}), bf16[4,512,1536]{2,1,0:T(8,128)(2,1)}) %all-gather.6.cloned.1.call-update) | async-done | bytes 6291472 | tf_op jit(solution)/shard_map/all_gather | solution.py:67
  271.6 2.6 convolution_add_fusion.16
  274.2 2.6 convolution_add_fusion.17
  278.8 2.1 convolution_add_fusion.19
  281.0 2.3 convert_bitcast_fusion.11
  287.9 5.6 %fusion.201 = f32[256,6144]{1,0:T(8,128)} fusion(pred[256,1024]{0,1:T(32,128)(4,1)S(1)} %copy-done.14, bf16[1024,6144]{1,0:T(8,128)(2,1)S(1)} %bitcast.106), kind=kOutput, calls=%fused_computation.299 | convolution fusion | flops 3221225472 | bytes 19136512 | tf_op jit(solution)/shard_map/dot_general | solution.py:32
  293.5 3.8 %convolution_add_fusion.1 = f32[256,6144]{1,0:T(8,128)S(1)} fusion(f32[256,6144]{1,0:T(8,128)} %fusion.201, bf16[18,6144]{1,0:T(8,128)(2,1)S(1)} %copy-done.4, s32[256]{0:T(256)S(1)} %bitcast.120), kind=kOutput, calls=%fused_computation.3 | convolution fusion | flops 58200576 | bytes 12805120 | tf_op jit(solution)/shard_map/dot_general | solution.py:32
  299.2 6.5 %fusion.202 = f32[256,6144]{1,0:T(8,128)} fusion(pred[256,1024]{0,1:T(32,128)(4,1)} %get-tuple-element.47, bf16[1024,6144]{1,0:T(8,128)(2,1)S(1)} %bitcast.106), kind=kOutput, calls=%fused_computation.300 | convolution fusion | flops 3221225472 | bytes 19136512 | tf_op jit(solution)/shard_map/dot_general | solution.py:32
  305.7 3.9 %convolution_add_fusion = f32[256,6144]{1,0:T(8,128)S(1)} fusion(f32[256,6144]{1,0:T(8,128)} %fusion.202, bf16[18,6144]{1,0:T(8,128)(2,1)S(1)} %copy-done.4, s32[256]{0:T(256)S(1)} %bitcast.119), kind=kOutput, calls=%fused_computation.2 | convolution fusion | flops 58200576 | bytes 12805120 | tf_op jit(solution)/shard_map/dot_general | solution.py:32
  320.6 5.3 %copy.27 = bf16[256,4,2048]{2,1,0:T(4,128)(2,1)} copy(bf16[256,4,2048]{2,0,1:T(8,128)(2,1)S(1)} %maximum_select_fusion) | data formatting | bytes 8388608
  325.8 5.6 %exponential_reduce_fusion = (f32[256,4,32]{0,2,1:T(8,128)S(1)}, f32[256,4,32]{0,2,1:T(8,128)S(1)}) fusion(s32[256,4,32]{0,2,1:T(8,128)S(1)} %copy-done.22, bf16[32,32,2048,1]{2,1,0,3:T(8,128)(2,1)S(1)} %bitcast.115, bf16[256,4,2048]{2,0,1:T(8,128)(2,1)S(1)} %maximum_select_fusion), kind=kOutput, calls=%fused_computation.9 | convolution fusion | flops 4299096064 | bytes 8781824 | tf_op jit(solution)/shard_map/dot_general | solution.py:90
  (118 shorter events, 29.7 us)
Async XLA Ops:
  7.2 20.6 %copy-start = (f32[256,2048]{1,0:T(8,128)S(1)}, f32[256,2048]{1,0:T(8,128)}, u32[]{:S(2)}) copy-start(f32[256,2048]{1,0:T(8,128)} %param.10) | copy-start | bytes 6291460
  7.2 76.0 %all-gather.8.cloned.1.call-start = ((), (), s32[]{:S(2)}) async-start(), calls=%async_computation.5 | async-start | bytes 4718592 | tf_op jit(solution)/shard_map/all_gather | solution.py:89
  7.9 198.7 %all-gather.4.cloned.1.call-start = ((), (), s32[]{:S(2)}) async-start(), calls=%async_computation.3 | async-start | bytes 14155776 | tf_op jit(solution)/shard_map/all_gather | solution.py:66
  8.7 262.9 %all-gather.6.cloned.1.call-start = ((), (), s32[]{:S(2)}) async-start(), calls=%async_computation.4 | async-start | bytes 7077888 | tf_op jit(solution)/shard_map/all_gather | solution.py:67
  10.8 14.4 %all-to-all-start = ((s32[32,1,8]{2,1,0:T(1,128)}), s32[32,1,8]{2,1,0:T(1,128)S(1)}, u32[]{:S(2)}, u32[]{:S(2)}) async-start(s32[32,1,8]{2,1,0:T(1,128)} %compare_convert_fusion), calls=%async_computation | async-start | bytes 32768 | tf_op jit(solution)/shard_map/all_to_all | solution.py:76
  25.2 10.2 %all-to-all-start.1 = ((s32[32,1,256]{2,1,0:T(1,128)}), s32[32,1,256]{2,1,0:T(1,128)S(1)}, u32[]{:S(2)}, u32[]{:S(2)}) async-start(s32[32,1,256]{2,1,0:T(1,128)} %reshape.433), calls=%async_computation.1 | async-start | bytes 65536 | tf_op jit(solution)/shard_map/all_to_all | solution.py:75
  30.5 7.8 %copy-start.23 = (s32[256,4]{0,1:T(4,128)S(1)}, s32[256,4]{0,1:T(4,128)}, u32[]{:S(2)}) copy-start(s32[256,4]{0,1:T(4,128)} %param.14) | copy-start | bytes 12292
  30.5 7.8 %copy-start.22 = (s32[256,4,32]{0,2,1:T(8,128)S(1)}, s32[256,4,32]{0,2,1:T(8,128)}, u32[]{:S(2)}) copy-start(s32[256,4,32]{0,2,1:T(8,128)} %param.15) | copy-start | bytes 393220
  35.4 189.2 %all-to-all-start.2 = ((f32[32,8,2048]{2,1,0:T(8,128)}), f32[32,8,2048]{2,1,0:T(8,128)S(1)}, u32[]{:S(2)}, u32[]{:S(2)}) async-start(f32[32,8,2048]{2,1,0:T(8,128)} %bitcast.114), calls=%async_computation.2 | async-start | bytes 4194304 | tf_op jit(solution)/shard_map/all_to_all | solution.py:74
  206.6 7.0 %copy-start.3 = (bf16[18,6144]{1,0:T(8,128)(2,1)S(1)}, bf16[18,6144]{1,0:T(8,128)(2,1)}, u32[]{:S(2)}) copy-start(bf16[18,6144]{1,0:T(8,128)(2,1)} %param.18) | copy-start | bytes 663556
  206.6 10.7 %slice-start = ((s8[12582912]{0:T(1024)(128)(4,1)}), s8[4194304]{0:T(1024)(128)(4,1)S(1)}, s32[]{:S(2)}) async-start(s8[12582912]{0:T(1024)(128)(4,1)} %bitcast.103), calls=%async_computation.6 | async-start | bytes 8388608
  206.6 10.7 %slice-start.1 = ((s8[12582912]{0:T(1024)(128)(4,1)}), s8[4194304]{0:T(1024)(128)(4,1)S(1)}, s32[]{:S(2)}) async-start(s8[12582912]{0:T(1024)(128)(4,1)} %bitcast.103), calls=%async_computation.7 | async-start | bytes 8388608
  213.6 3.7 %slice-start.2 = ((s8[12582912]{0:T(1024)(128)(4,1)}), s8[4194304]{0:T(1024)(128)(4,1)S(1)}, s32[]{:S(2)}) async-start(s8[12582912]{0:T(1024)(128)(4,1)} %bitcast.103), calls=%async_computation.8 | async-start | bytes 8388608
  271.6 5.2 %copy-start.2 = (bf16[4,512,1536]{2,1,0:T(8,128)(2,1)S(1)}, bf16[4,512,1536]{2,1,0:T(8,128)(2,1)}, u32[]{:S(2)}) copy-start(bf16[4,512,1536]{2,1,0:T(8,128)(2,1)} %all-gather.6.cloned.1.call-done) | copy-start | bytes 18874372
  274.2 9.1 %slice-start.6 = ((s8[6291456]{0:T(1024)(128)(4,1)}), s8[4194304]{0:T(1024)(128)(4,1)S(1)}, s32[]{:S(2)}) async-start(s8[6291456]{0:T(1024)(128)(4,1)} %bitcast.107), calls=%async_computation.12 | async-start | bytes 8388608
  278.8 4.5 %slice-start.7 = ((s8[6291456]{0:T(1024)(128)(4,1)}), s8[2097152]{0:T(1024)(128)(4,1)S(1)}, s32[]{:S(2)}) async-start(s8[6291456]{0:T(1024)(128)(4,1)} %bitcast.107), calls=%async_computation.13 | async-start | bytes 4194304
  280.9 6.9 %slice-start.3 = ((s8[12582912]{0:T(1024)(128)(4,1)}), s8[4194304]{0:T(1024)(128)(4,1)S(1)}, s32[]{:S(2)}) async-start(s8[12582912]{0:T(1024)(128)(4,1)} %bitcast.105), calls=%async_computation.9 | async-start | bytes 8388608
  281.0 6.9 %slice-start.4 = ((s8[12582912]{0:T(1024)(128)(4,1)}), s8[4194304]{0:T(1024)(128)(4,1)S(1)}, s32[]{:S(2)}) async-start(s8[12582912]{0:T(1024)(128)(4,1)} %bitcast.105), calls=%async_computation.10 | async-start | bytes 8388608
  285.2 2.6 slice-start.5
  287.9 5.6 %copy-start.4 = (bf16[18,6144]{1,0:T(8,128)(2,1)S(1)}, bf16[18,6144]{1,0:T(8,128)(2,1)}, u32[]{:S(2)}) copy-start(bf16[18,6144]{1,0:T(8,128)(2,1)} %param.18) | copy-start | bytes 663556
  293.5 3.9 %copy-start.12 = (f32[256,512]{1,0:T(8,128)S(1)}, f32[256,512]{1,0:T(8,128)}, u32[]{:S(2)}) copy-start(f32[256,512]{1,0:T(8,128)} %get-tuple-element.54) | copy-start | bytes 1572868
  305.7 3.9 %copy-start.10 = (f32[256,512]{1,0:T(8,128)S(1)}, f32[256,512]{1,0:T(8,128)}, u32[]{:S(2)}) copy-start(f32[256,512]{1,0:T(8,128)} %get-tuple-element.27) | copy-start | bytes 1572868
  320.6 5.3 %copy-start.13 = (bf16[1024,2048]{1,0:T(8,128)(2,1)S(1)}, bf16[1024,2048]{1,0:T(8,128)(2,1)}, u32[]{:S(2)}) copy-start(bf16[1024,2048]{1,0:T(8,128)(2,1)} %copy.26) | copy-start | bytes 12582916
  325.8 6.3 %copy-start.1 = (f32[256,2048]{1,0:T(8,128)S(1)}, f32[256,2048]{1,0:T(8,128)}, u32[]{:S(2)}) copy-start(f32[256,2048]{1,0:T(8,128)} %param.10) | copy-start | bytes 6291460
  (14 other events, 16.8 us)
Sparse Core Ops, SparseCore 0:
  9.6 73.5 all-gather.7
  84.8 121.7 all-gather.3
  208.2 63.3 all-gather.5
where the time goes:
time: 339 us
  waiting for transfers between devices  217 us (64%)
  matrix products  59.7 us (18%)
  local copies, waits for them, and re-layouts  20.3 us (6%)
  other arithmetic  15 us (4%)
  between operations  14.3 us (4%)
  starting transfers between devices  12.7 us (4%)
    all_gather x1, waiting for transfers between devices, on_device(): stoch_full = lax.all_gather(w_stoch, 'gy', axis=0, tiled=True)  117 us
    all_gather x1, waiting for transfers between devices, on_device(): deter_full = lax.all_gather(w_deter, 'gy', axis=1, tiled=True)  47 us
    all_gather x1, waiting for transfers between devices, on_device(): prior_full = lax.all_gather(w_prior, 'gy', axis=0, tiled=True)  41.9 us
    dot_general x4, matrix products, imagine(): jnp.dot(onehot, stoch_full, preferred_element_type=jnp.float32)  22.7 us
    dot_general x16, matrix products, imagine(): jnp.dot(before.astype(jnp.bfloat16), deter_full[b], preferred_element_typ...  16.3 us
    dot_general x4, matrix products, imagine(): jnp.dot(act_hot, act_table, preferred_element_type=jnp.float32)  15 us
    unnamed x68, local copies, waits for them, and re-layouts  9.44 us
    concatenate x11, other arithmetic, imagine(): states.append(jnp.concatenate(pieces, 1).astype(jnp.bfloat16))  8.3 us
  transfers between devices with their start and end apart: 6, of which 5 were waited for; matrix products, arithmetic and copies ran while one was open for 10% of the time, Pallas kernels for 0%

commit v1 on v0

--- a/solution.py
+++ b/solution.py
@@ -86,7 +86,27 @@
         act_table,
     )
     states = jnp.where(live[:, None, None] > 0, states, jnp.zeros_like(states))
-    prior_full = lax.all_gather(w_prior, "gy", axis=0, tiled=True)
+    moved = lax.psum(1, axis_name="gy")
+    view_out = lax.axis_index("gy")
+    tmp, f_next, local_out = (moved, view_out, w_prior.shape[0])
+    gallery = tuple(((k0, (k0 + 1) % tmp) for k0 in range(tmp)))
+    pages = tuple(((k0, (k0 - 1) % tmp) for k0 in range(tmp)))
+    prior_full = jnp.zeros(
+        (*w_prior.shape[:0], tmp * local_out, *w_prior.shape[0 + 1 :]), w_prior.dtype
+    )
+    prior_full = lax.dynamic_update_slice_in_dim(prior_full, w_prior, f_next * local_out, axis=0)
+    then = left_arr = w_prior
+    y2 = tmp // 2
+    for nth in [*range(1, y2 + 1)]:
+        then = lax.ppermute(then, axis_name="gy", perm=gallery)
+        prior_full = lax.dynamic_update_slice_in_dim(
+            prior_full, then, (f_next - nth) % tmp * local_out, axis=0
+        )
+        if nth < tmp - y2:
+            left_arr = lax.ppermute(left_arr, "gy", pages)
+            prior_full = lax.dynamic_update_slice_in_dim(
+                prior_full, left_arr, (f_next + nth) % tmp * local_out, axis=0
+            )
     logits = jnp.dot(
         states.reshape(slots * STEPS, deter), prior_full, preferred_element_type=jnp.float32
     )

time: 339 us -> 349 us (1.029); the launches traced: 339 us -> 343 us
  waiting for transfers between devices: 217 us -> 145 us
  starting transfers between devices: 12.7 us -> 60.2 us
  matrix products: 59.7 us -> 75.2 us
  local copies, waits for them, and re-layouts: 20.3 us -> 33 us
    all_gather x1, waiting for transfers between devices: 117 us -> 1.18 us  [on_device(): stoch_full = lax.all_gather(w_stoch, 'gy', axis=0, tiled=True)]
    ppermute x0 -> x7, waiting for transfers between devices: none -> 86.3 us  [the longest x3 67.6 us: on_device(): left_arr = lax.ppermute(left_arr, 'gy', pages)]
    all_gather x1 -> x0, waiting for transfers between devices: 41.9 us -> none  [on_device(): prior_full = lax.all_gather(w_prior, 'gy', axis=0, tiled=True)]
    all_to_all x1, starting transfers between devices: 2.57 us -> 22.8 us  [on_device(): lax.all_to_all(first, ('gx', 'gy'), split_axis=0, concat_axis=0, tiled=True)]
    all_to_all x1, starting transfers between devices: 2.73 us -> 21.1 us  [on_device(): lax.all_to_all(start, ('gx', 'gy'), split_axis=0, concat_axis=0, tiled=True)]
    dot_general x4, matrix products: 22.7 us -> 34.9 us  [imagine(): jnp.dot(onehot, stoch_full, preferred_element_type=jnp.float32)]
    ppermute x0 -> x7, starting transfers between devices: none -> 11.7 us  [the longest x3 11.2 us: on_device(): left_arr = lax.ppermute(left_arr, 'gy', pages)]
    ppermute x0 -> x7, local copies, waits for them, and re-layouts: none -> 8.71 us  [the longest x4 4.98 us: on_device(): then = lax.ppermute(then, axis_name='gy', perm=gallery)]
  transfers between devices with their start and end apart: 6 -> 12, of which waited for: 5 -> 7; matrix products, arithmetic and copies ran while one was open for 10% -> 14% of each run, Pallas kernels for 0% -> 0%
where the time goes in v1:
time: 349 us; the launch traced here: 343 us
  waiting for transfers between devices  145 us (42%)
  matrix products  75.2 us (22%)
  starting transfers between devices  60.2 us (17%)
  local copies, waits for them, and re-layouts  33 us (9%)
  between operations  14.9 us (4%)
  other arithmetic  14.8 us (4%)
    ppermute x3, waiting for transfers between devices, on_device(): left_arr = lax.ppermute(left_arr, 'gy', pages)  67.6 us
    all_gather x1, waiting for transfers between devices, on_device(): deter_full = lax.all_gather(w_deter, 'gy', axis=1, tiled=True)  48.1 us
    dot_general x4, matrix products, imagine(): jnp.dot(onehot, stoch_full, preferred_element_type=jnp.float32)  34.9 us
    all_to_all x1, starting transfers between devices, on_device(): lax.all_to_all(first, ('gx', 'gy'), split_axis=0, concat_axis=0, tiled=True)  22.8 us
    all_to_all x1, starting transfers between devices, on_device(): lax.all_to_all(start, ('gx', 'gy'), split_axis=0, concat_axis=0, tiled=True)  21.1 us
    ppermute x4, waiting for transfers between devices, on_device(): then = lax.ppermute(then, axis_name='gy', perm=gallery)  18.7 us
    dot_general x16, matrix products, imagine(): jnp.dot(before.astype(jnp.bfloat16), deter_full[b], preferred_element_typ...  16.3 us
    dot_general x4, matrix products, imagine(): jnp.dot(act_hot, act_table, preferred_element_type=jnp.float32)  15.6 us
  transfers between devices with their start and end apart: 12, of which 7 were waited for; matrix products, arithmetic and copies ran while one was open for 14% of the time, Pallas kernels for 0%

profile of v1, /device:TPU:0, one launch (start us, length us, event | category | flops | bytes accessed | tf_op | source)
XLA Modules:
  0.0 343.0 jit_solution(3446384621733141348)
XLA Ops:
  9.2 4.1 %collective-permute-start.1 = (bf16[256,1024]{1,0:T(8,128)(2,1)}, bf16[256,1024]{1,0:T(8,128)(2,1)}, u32[]{:S(2)}, u32[]{:S(2)}) collective-permute-start(bf16[256,1024]{1,0:T(8,128)(2,1)} %param.19), channel_id=1, source_target_pairs={{0,7},{1,0},{2,1},{3,2},{4,3},{5,4},{6,5},{7,6},{8,15},{9,8},{10,9... | collective-permute-start | bytes 1572872 | tf_op jit(solution)/shard_map/ppermute | solution.py:106
  14.7 4.5 %all-to-all-start = ((s32[32,1,8]{2,1,0:T(1,128)}), s32[32,1,8]{2,1,0:T(1,128)S(1)}, u32[]{:S(2)}, u32[]{:S(2)}) async-start(s32[32,1,8]{2,1,0:T(1,128)} %compare_convert_fusion), calls=%async_computation | async-start | bytes 32768 | tf_op jit(solution)/shard_map/all_to_all | solution.py:76
  19.2 4.3 %collective-permute-done = bf16[256,1024]{1,0:T(8,128)(2,1)} collective-permute-done((bf16[256,1024]{1,0:T(8,128)(2,1)}, bf16[256,1024]{1,0:T(8,128)(2,1)}, u32[]{:S(2)}, u32[]{:S(2)}) %collective-permute-start) | collective-permute-done | bytes 524320 | tf_op jit(solution)/shard_map/ppermute | solution.py:101
  24.3 4.7 %collective-permute-done.1 = bf16[256,1024]{1,0:T(8,128)(2,1)} collective-permute-done((bf16[256,1024]{1,0:T(8,128)(2,1)}, bf16[256,1024]{1,0:T(8,128)(2,1)}, u32[]{:S(2)}, u32[]{:S(2)}) %collective-permute-start.1) | collective-permute-done | bytes 524320 | tf_op jit(solution)/shard_map/ppermute | solution.py:106
  29.0 3.7 %collective-permute-start.3 = (bf16[256,1024]{1,0:T(8,128)(2,1)}, bf16[256,1024]{1,0:T(8,128)(2,1)}, u32[]{:S(2)}, u32[]{:S(2)}) collective-permute-start(bf16[256,1024]{1,0:T(8,128)(2,1)} %collective-permute-done.1), channel_id=1, source_target_pairs={{0,7},{1,0},{2,1},{3,2},{4,3},{5,4},{6,5},{7,6},{8,15},{9,8},{10,9... | collective-permute-start | bytes 1572872 | tf_op jit(solution)/shard_map/ppermute | solution.py:106
  35.9 14.4 %collective-permute-done.2 = bf16[256,1024]{1,0:T(8,128)(2,1)} collective-permute-done((bf16[256,1024]{1,0:T(8,128)(2,1)}, bf16[256,1024]{1,0:T(8,128)(2,1)}, u32[]{:S(2)}, u32[]{:S(2)}) %collective-permute-start.2) | collective-permute-done | bytes 524320 | tf_op jit(solution)/shard_map/ppermute | solution.py:101
  50.4 22.8 %all-to-all-start.1 = ((s32[32,1,256]{2,1,0:T(1,128)}), s32[32,1,256]{2,1,0:T(1,128)S(1)}, u32[]{:S(2)}, u32[]{:S(2)}) async-start(s32[32,1,256]{2,1,0:T(1,128)} %reshape.433), calls=%async_computation.1 | async-start | bytes 65536 | tf_op jit(solution)/shard_map/all_to_all | solution.py:75
  73.4 2.7 gather_fusion.1
  76.1 7.9 %all-to-all-done.1 = s32[32,1,256]{2,1,0:T(1,128)S(1)} async-done(((s32[32,1,256]{2,1,0:T(1,128)}), s32[32,1,256]{2,1,0:T(1,128)S(1)}, u32[]{:S(2)}, u32[]{:S(2)}) %all-to-all-start.1) | async-done | bytes 32800 | tf_op jit(solution)/shard_map/all_to_all | solution.py:75
  84.0 21.1 %all-to-all-start.2 = ((f32[32,8,2048]{2,1,0:T(8,128)}), f32[32,8,2048]{2,1,0:T(8,128)S(1)}, u32[]{:S(2)}, u32[]{:S(2)}) async-start(f32[32,8,2048]{2,1,0:T(8,128)} %bitcast.115), calls=%async_computation.2 | async-start | bytes 4194304 | tf_op jit(solution)/shard_map/all_to_all | solution.py:74
  108.6 3.4 collective-permute-start.5
  124.8 62.9 %collective-permute-done.5 = bf16[256,1024]{1,0:T(8,128)(2,1)} collective-permute-done((bf16[256,1024]{1,0:T(8,128)(2,1)}, bf16[256,1024]{1,0:T(8,128)(2,1)}, u32[]{:S(2)}, u32[]{:S(2)}) %collective-permute-start.5) | collective-permute-done | bytes 524320 | tf_op jit(solution)/shard_map/ppermute | solution.py:106
  194.0 7.2 %fusion.199 = f32[256,6144]{1,0:T(8,128)S(1)} fusion(pred[256,1024]{0,1:T(32,128)(4,1)} %get-tuple-element.50, bf16[1024,6144]{1,0:T(8,128)(2,1)} %all-gather.3.cloned.1.call-done), kind=kOutput, calls=%fused_computation.305 | convolution fusion | flops 3221225472 | bytes 19136512 | tf_op jit(solution)/shard_map/dot_general | solution.py:32
  201.3 4.2 %convolution_add_fusion.3 = f32[256,6144]{1,0:T(8,128)} fusion(f32[256,6144]{1,0:T(8,128)S(1)} %fusion.199, bf16[18,6144]{1,0:T(8,128)(2,1)S(1)} %copy-done.3, s32[256]{0:T(256)S(1)} %bitcast.121), kind=kOutput, calls=%fused_computation.5 | convolution fusion | flops 58200576 | bytes 12805120 | tf_op jit(solution)/shard_map/dot_general | solution.py:32
  205.4 3.6 %fusion.200 = f32[256,6144]{1,0:T(8,128)S(1)} fusion(pred[256,1024]{0,1:T(32,128)(4,1)S(1)} %get-tuple-element.48, bf16[1024,6144]{1,0:T(8,128)(2,1)S(1)} %bitcast.105), kind=kOutput, calls=%fused_computation.306 | convolution fusion | flops 3221225472 | bytes 19136512 | tf_op jit(solution)/shard_map/dot_general | solution.py:32
  209.1 3.7 %convolution_add_fusion.2 = f32[256,6144]{1,0:T(8,128)} fusion(f32[256,6144]{1,0:T(8,128)S(1)} %fusion.200, bf16[18,6144]{1,0:T(8,128)(2,1)S(1)} %copy-done.3, s32[256]{0:T(256)S(1)} %bitcast.120), kind=kOutput, calls=%fused_computation.4 | convolution fusion | flops 58200576 | bytes 12805120 | tf_op jit(solution)/shard_map/dot_general | solution.py:32
  212.8 48.1 %all-gather.5.cloned.1.call-done = bf16[4,512,1536]{2,1,0:T(8,128)(2,1)} async-done(((bf16[4,64,1536]{2,1,0:T(8,128)(2,1)}), bf16[4,512,1536]{2,1,0:T(8,128)(2,1)}) %all-gather.5.cloned.1.call-update) | async-done | bytes 6291472 | tf_op jit(solution)/shard_map/all_gather | solution.py:67
  263.5 2.6 convolution_add_fusion.17
  277.2 17.5 %fusion.201 = f32[256,6144]{1,0:T(8,128)} fusion(pred[256,1024]{0,1:T(32,128)(4,1)S(1)} %copy-done.13, bf16[1024,6144]{1,0:T(8,128)(2,1)S(1)} %bitcast.107), kind=kOutput, calls=%fused_computation.307 | convolution fusion | flops 3221225472 | bytes 19136512 | tf_op jit(solution)/shard_map/dot_general | solution.py:32
  294.7 3.8 %convolution_add_fusion.1 = f32[256,6144]{1,0:T(8,128)S(1)} fusion(f32[256,6144]{1,0:T(8,128)} %fusion.201, bf16[18,6144]{1,0:T(8,128)(2,1)S(1)} %copy-done.4, s32[256]{0:T(256)S(1)} %bitcast.119), kind=kOutput, calls=%fused_computation.3 | convolution fusion | flops 58200576 | bytes 12805120 | tf_op jit(solution)/shard_map/dot_general | solution.py:32
  300.4 6.6 %fusion.202 = f32[256,6144]{1,0:T(8,128)} fusion(pred[256,1024]{0,1:T(32,128)(4,1)} %get-tuple-element.47, bf16[1024,6144]{1,0:T(8,128)(2,1)S(1)} %bitcast.107), kind=kOutput, calls=%fused_computation.308 | convolution fusion | flops 3221225472 | bytes 19136512 | tf_op jit(solution)/shard_map/dot_general | solution.py:32
  307.0 3.9 %convolution_add_fusion = f32[256,6144]{1,0:T(8,128)S(1)} fusion(f32[256,6144]{1,0:T(8,128)} %fusion.202, bf16[18,6144]{1,0:T(8,128)(2,1)S(1)} %copy-done.4, s32[256]{0:T(256)S(1)} %bitcast.118), kind=kOutput, calls=%fused_computation.2 | convolution fusion | flops 58200576 | bytes 12805120 | tf_op jit(solution)/shard_map/dot_general | solution.py:32
  321.6 5.3 %copy.48 = bf16[256,4,2048]{2,1,0:T(4,128)(2,1)} copy(bf16[256,4,2048]{2,0,1:T(8,128)(2,1)S(1)} %maximum_select_fusion) | data formatting | bytes 8388608
  326.9 8.3 %exponential_reduce_fusion = (f32[256,4,32]{0,2,1:T(8,128)S(1)}, f32[256,4,32]{0,2,1:T(8,128)S(1)}) fusion(s32[256,4,32]{0,2,1:T(8,128)S(1)} %copy-done.22, bf16[32,32,2048,1]{2,1,0,3:T(8,128)(2,1)} %bitcast.40, bf16[256,4,2048]{2,0,1:T(8,128)(2,1)S(1)} %maximum_select_fusion), kind=kOutput, calls=%fused_computation.9 | convolution fusion | flops 4299096064 | bytes 8781824 | tf_op jit(solution)/shard_map/dot_general | solution.py:110
  (145 shorter events, 56.8 us)
Async XLA Ops:
  7.2 66.3 %copy-start = (f32[256,2048]{1,0:T(8,128)S(1)}, f32[256,2048]{1,0:T(8,128)}, u32[]{:S(2)}) copy-start(f32[256,2048]{1,0:T(8,128)} %param.10) | copy-start | bytes 6291460
  7.2 66.0 %copy-start.21 = (bf16[256,1024]{1,0:T(8,128)(2,1)S(1)}, bf16[256,1024]{1,0:T(8,128)(2,1)}, u32[]{:S(2)}) copy-start(bf16[256,1024]{1,0:T(8,128)(2,1)} %param.19) | copy-start | bytes 1572868
  7.2 66.0 %copy-start.23 = (s32[256,4]{0,1:T(4,128)S(1)}, s32[256,4]{0,1:T(4,128)}, u32[]{:S(2)}) copy-start(s32[256,4]{0,1:T(4,128)} %param.14) | copy-start | bytes 12292
  7.2 186.8 %all-gather.3.cloned.1.call-start = ((), (), s32[]{:S(2)}) async-start(), calls=%async_computation.3 | async-start | bytes 14155776 | tf_op jit(solution)/shard_map/all_gather | solution.py:66
  7.9 253.0 %all-gather.5.cloned.1.call-start = ((), (), s32[]{:S(2)}) async-start(), calls=%async_computation.4 | async-start | bytes 7077888 | tf_op jit(solution)/shard_map/all_gather | solution.py:67
  8.7 14.8 %collective-permute-start = (bf16[256,1024]{1,0:T(8,128)(2,1)}, bf16[256,1024]{1,0:T(8,128)(2,1)}, u32[]{:S(2)}, u32[]{:S(2)}) collective-permute-start(bf16[256,1024]{1,0:T(8,128)(2,1)} %param.19), channel_id=1, source_target_pairs={{0,1},{1,2},{2,3},{3,4},{4,5},{5,6},{6,7},{7,0},{8,9},{9,10},{10,1... | collective-permute-start | bytes 1572872 | tf_op jit(solution)/shard_map/ppermute | solution.py:101
  9.2 19.8 %collective-permute-start.1 = (bf16[256,1024]{1,0:T(8,128)(2,1)}, bf16[256,1024]{1,0:T(8,128)(2,1)}, u32[]{:S(2)}, u32[]{:S(2)}) collective-permute-start(bf16[256,1024]{1,0:T(8,128)(2,1)} %param.19), channel_id=1, source_target_pairs={{0,7},{1,0},{2,1},{3,2},{4,3},{5,4},{6,5},{7,6},{8,15},{9,8},{10,9... | collective-permute-start | bytes 1572872 | tf_op jit(solution)/shard_map/ppermute | solution.py:106
  14.7 35.7 %all-to-all-start = ((s32[32,1,8]{2,1,0:T(1,128)}), s32[32,1,8]{2,1,0:T(1,128)S(1)}, u32[]{:S(2)}, u32[]{:S(2)}) async-start(s32[32,1,8]{2,1,0:T(1,128)} %compare_convert_fusion), calls=%async_computation | async-start | bytes 32768 | tf_op jit(solution)/shard_map/all_to_all | solution.py:76
  23.5 26.9 %collective-permute-start.2 = (bf16[256,1024]{1,0:T(8,128)(2,1)}, bf16[256,1024]{1,0:T(8,128)(2,1)}, u32[]{:S(2)}, u32[]{:S(2)}) collective-permute-start(bf16[256,1024]{1,0:T(8,128)(2,1)} %collective-permute-done), channel_id=1, source_target_pairs={{0,1},{1,2},{2,3},{3,4},{4,5},{5,6},{6,7},{7,0},{8,9},{9,10},{10,1... | collective-permute-start | bytes 1572872 | tf_op jit(solution)/shard_map/ppermute | solution.py:101
  29.0 79.6 %collective-permute-start.3 = (bf16[256,1024]{1,0:T(8,128)(2,1)}, bf16[256,1024]{1,0:T(8,128)(2,1)}, u32[]{:S(2)}, u32[]{:S(2)}) collective-permute-start(bf16[256,1024]{1,0:T(8,128)(2,1)} %collective-permute-done.1), channel_id=1, source_target_pairs={{0,7},{1,0},{2,1},{3,2},{4,3},{5,4},{6,5},{7,6},{8,15},{9,8},{10,9... | collective-permute-start | bytes 1572872 | tf_op jit(solution)/shard_map/ppermute | solution.py:106
  50.3 68.1 %collective-permute-start.4 = (bf16[256,1024]{1,0:T(8,128)(2,1)}, bf16[256,1024]{1,0:T(8,128)(2,1)}, u32[]{:S(2)}, u32[]{:S(2)}) collective-permute-start(bf16[256,1024]{1,0:T(8,128)(2,1)} %collective-permute-done.2), channel_id=1, source_target_pairs={{0,1},{1,2},{2,3},{3,4},{4,5},{5,6},{6,7},{7,0},{8,9},{9,10},{10,1... | collective-permute-start | bytes 1572872 | tf_op jit(solution)/shard_map/ppermute | solution.py:101
  50.4 33.7 %all-to-all-start.1 = ((s32[32,1,256]{2,1,0:T(1,128)}), s32[32,1,256]{2,1,0:T(1,128)S(1)}, u32[]{:S(2)}, u32[]{:S(2)}) async-start(s32[32,1,256]{2,1,0:T(1,128)} %reshape.433), calls=%async_computation.1 | async-start | bytes 65536 | tf_op jit(solution)/shard_map/all_to_all | solution.py:75
  84.0 128.8 %all-to-all-start.2 = ((f32[32,8,2048]{2,1,0:T(8,128)}), f32[32,8,2048]{2,1,0:T(8,128)S(1)}, u32[]{:S(2)}, u32[]{:S(2)}) async-start(f32[32,8,2048]{2,1,0:T(8,128)} %bitcast.115), calls=%async_computation.2 | async-start | bytes 4194304 | tf_op jit(solution)/shard_map/all_to_all | solution.py:74
  108.6 79.1 %collective-permute-start.5 = (bf16[256,1024]{1,0:T(8,128)(2,1)}, bf16[256,1024]{1,0:T(8,128)(2,1)}, u32[]{:S(2)}, u32[]{:S(2)}) collective-permute-start(bf16[256,1024]{1,0:T(8,128)(2,1)} %collective-permute-done.3), channel_id=1, source_target_pairs={{0,7},{1,0},{2,1},{3,2},{4,3},{5,4},{6,5},{7,6},{8,15},{9,8},{10,9... | collective-permute-start | bytes 1572872 | tf_op jit(solution)/shard_map/ppermute | solution.py:106
  118.5 72.3 %collective-permute-start.6 = (bf16[256,1024]{1,0:T(8,128)(2,1)}, bf16[256,1024]{1,0:T(8,128)(2,1)}, u32[]{:S(2)}, u32[]{:S(2)}) collective-permute-start(bf16[256,1024]{1,0:T(8,128)(2,1)} %collective-permute-done.4), channel_id=1, source_target_pairs={{0,1},{1,2},{2,3},{3,4},{4,5},{5,6},{6,7},{7,0},{8,9},{9,10},{10,1... | collective-permute-start | bytes 1572872 | tf_op jit(solution)/shard_map/ppermute | solution.py:101
  194.0 7.2 %copy-start.3 = (bf16[18,6144]{1,0:T(8,128)(2,1)S(1)}, bf16[18,6144]{1,0:T(8,128)(2,1)}, u32[]{:S(2)}) copy-start(bf16[18,6144]{1,0:T(8,128)(2,1)} %param.18) | copy-start | bytes 663556
  194.0 11.4 %slice-start = ((s8[12582912]{0:T(1024)(128)(4,1)}), s8[4194304]{0:T(1024)(128)(4,1)S(1)}, s32[]{:S(2)}) async-start(s8[12582912]{0:T(1024)(128)(4,1)} %bitcast.104), calls=%async_computation.5 | async-start | bytes 8388608
  194.0 11.4 %slice-start.1 = ((s8[12582912]{0:T(1024)(128)(4,1)}), s8[4194304]{0:T(1024)(128)(4,1)S(1)}, s32[]{:S(2)}) async-start(s8[12582912]{0:T(1024)(128)(4,1)} %bitcast.104), calls=%async_computation.6 | async-start | bytes 8388608
  263.5 9.1 %slice-start.6 = ((s8[6291456]{0:T(1024)(128)(4,1)}), s8[4194304]{0:T(1024)(128)(4,1)S(1)}, s32[]{:S(2)}) async-start(s8[6291456]{0:T(1024)(128)(4,1)} %bitcast.108), calls=%async_computation.11 | async-start | bytes 8388608
  270.3 6.9 %slice-start.3 = ((s8[12582912]{0:T(1024)(128)(4,1)}), s8[4194304]{0:T(1024)(128)(4,1)S(1)}, s32[]{:S(2)}) async-start(s8[12582912]{0:T(1024)(128)(4,1)} %bitcast.106), calls=%async_computation.8 | async-start | bytes 8388608
  270.3 6.9 %slice-start.4 = ((s8[12582912]{0:T(1024)(128)(4,1)}), s8[4194304]{0:T(1024)(128)(4,1)S(1)}, s32[]{:S(2)}) async-start(s8[12582912]{0:T(1024)(128)(4,1)} %bitcast.106), calls=%async_computation.9 | async-start | bytes 8388608
  277.2 17.5 %copy-start.4 = (bf16[18,6144]{1,0:T(8,128)(2,1)S(1)}, bf16[18,6144]{1,0:T(8,128)(2,1)}, u32[]{:S(2)}) copy-start(bf16[18,6144]{1,0:T(8,128)(2,1)} %param.18) | copy-start | bytes 663556
  321.6 5.3 %copy-start.22 = (s32[256,4,32]{0,2,1:T(8,128)S(1)}, s32[256,4,32]{0,2,1:T(8,128)}, u32[]{:S(2)}) copy-start(s32[256,4,32]{0,2,1:T(8,128)} %param.15) | copy-start | bytes 393220
  326.9 9.0 %copy-start.1 = (f32[256,2048]{1,0:T(8,128)S(1)}, f32[256,2048]{1,0:T(8,128)}, u32[]{:S(2)}) copy-start(f32[256,2048]{1,0:T(8,128)} %param.10) | copy-start | bytes 6291460
  (20 other events, 41.0 us)
Sparse Core Ops, SparseCore 0:
  9.7 184.3 all-gather.2
  195.6 65.2 all-gather.4
